TPU v7x, 32 devices: a whole 2x2x4 slice. The times are simulated.
32 devices in a mesh: trade: 4 (over z), node: 8 (over y, x, core).
Axes of the slice: x: 2, y: 2, z: 4, core: 2. Of those that a mesh axis runs over, the one named last changes fastest.
Arguments:
- values_in: float32 [1024, 16384], P('trade', 'node'), may hold values from 0 to 1
- prob_up: float32 [16, 16384], P(None, 'node'), may hold values from 0.1 to 0.3
- prob_down: float32 [16, 16384], P(None, 'node'), may hold values from 0.1 to 0.3
- discount: float32 [16, 16384], P(None, 'node'), may hold values from 0.9 to 1
- swap_rate: float32 [16, 16384], P(None, 'node'), may hold values from -3 to 3
- annuity: float32 [16, 16384], P(None, 'node'), may hold values from 0.5 to 2
- state_price: float32 [16384], P('node'), may hold values from 3.0517578e-05 to 0.00012207031
- exercise_step: int32 [1024, 4], P('trade'), may hold values from 0 to 15
- strike_bucket: int32 [1024], P('trade'), may hold values from 0 to 63
- notional_sign: int32 [1024], P('trade'), may hold values from 0 to 1
- strike_table: float32 [64], replicated, may hold values from -0.5 to 0.5
Outputs:
- values_out: float32 [1024, 16384], P(('trade', 'node'))
- prices: float32 [1024], P(('trade', 'node'))
- portfolio: float32 [], replicated
All inputs are finite; a program needn't handle non-finite values.
Results may differ from a plain program's by a relative error of at most 0.0003.
Values sent between devices are 32-bit elements; how exact they have to be, the bound alone decides.
A program may use at most 128 MiB of HBM per device.

v0:
```python
import jax
import jax.numpy as jnp
from jax import lax
from jax.sharding import PartitionSpec as P


def strikes_of(bucket, strike_table):
    levels = lax.broadcasted_iota(jnp.int32, (1, strike_table.shape[0]), 1)
    return jnp.sum(
        jnp.where(
            bucket[:, None] == levels, strike_table[None, :], jnp.zeros((), strike_table.dtype)
        ),
        axis=1,
    )


def roll_once(padded, prob_up, prob_down, discount_row):
    middle = 1.0 - prob_up - prob_down
    return discount_row * (
        prob_up * padded[:, 2:] + middle * padded[:, 1:-1] + prob_down * padded[:, :-2]
    )


def exercise(values, active, strike, signs, swap_row, annuity_row):
    payoff = signs[:, None] * annuity_row[None, :] * (swap_row[None, :] - strike[:, None])
    return jnp.where(active[:, None], jnp.maximum(values, payoff), values)


def stack_lattice(prob_up, prob_down, discount, swap_rate, annuity, state_price, first_step):
    span = prob_up.shape[0] - first_step
    spread_price = jnp.broadcast_to(state_price[None, :], (span, state_price.shape[0]))
    return jnp.stack([prob_up, prob_down, discount, swap_rate, annuity, spread_price])


def to_trade_rows(values):
    node_count = lax.axis_size("node")
    node_dev = values.shape[1]
    row_count = values.shape[0] // node_count
    blocks = values.reshape(node_count, row_count, node_dev)
    moved = lax.all_to_all(blocks, "node", split_axis=0, concat_axis=2, tiled=True)
    return moved.reshape(row_count, node_dev * node_count)


def roll_back(values, lattice, exercise_step, strike, signs, split_step, step_count):
    row_count = values.shape[0]
    first_row = lax.axis_index("node") * row_count
    my_dates = lax.dynamic_slice_in_dim(exercise_step, first_row, row_count, 0)
    my_strike = lax.dynamic_slice_in_dim(strike, first_row, row_count, 0)
    my_signs = lax.dynamic_slice_in_dim(signs, first_row, row_count, 0)
    for step in range(split_step, step_count):
        local_step = step - split_step
        padded = jnp.pad(values, ((0, 0), (1, 1)))
        values = roll_once(
            padded, lattice[0, local_step], lattice[1, local_step], lattice[2, local_step]
        )
        active = jnp.any(my_dates == step, axis=1)
        values = exercise(
            values, active, my_strike, my_signs, lattice[3, local_step], lattice[4, local_step]
        )
    prices = jnp.sum(values * lattice[5, 0][None, :], axis=1)
    return (values, prices)


def local(
    values_in,
    prob_up,
    prob_down,
    discount,
    swap_rate,
    annuity,
    state_price,
    exercise_step,
    strike_bucket,
    notional_sign,
    strike_table,
):
    step_count = prob_up.shape[0]
    strike = strikes_of(strike_bucket, strike_table)
    signs = (2 * notional_sign - 1).astype(jnp.float32)
    values = to_trade_rows(values_in)
    local_lattice = stack_lattice(prob_up, prob_down, discount, swap_rate, annuity, state_price, 0)
    lattice = lax.all_gather(local_lattice, "node", axis=2, tiled=True)
    values, prices = roll_back(values, lattice, exercise_step, strike, signs, 0, step_count)
    portfolio = lax.psum(jnp.sum(prices), ("trade", "node")) / values_in.shape[0]
    return (values, prices, portfolio)


def solution(mesh):
    in_specs = (
        P("trade", "node"),
        P(None, "node"),
        P(None, "node"),
        P(None, "node"),
        P(None, "node"),
        P(None, "node"),
        P("node"),
        P("trade", None),
        P("trade"),
        P("trade"),
        P(),
    )
    out_specs = (P(("trade", "node"), None), P(("trade", "node")), P())
    return jax.shard_map(local, mesh=mesh, in_specs=in_specs, out_specs=out_specs, check_vma=False)
```

profile of v0, /device:TPU:0, one launch (start us, length us, event | category | flops | bytes accessed | tf_op | source)
XLA Modules:
  0.0 175.1 jit_solution(9109322315187114257)
XLA Ops:
  7.2 0.0 all-gather.2.cloned.1.call-start
  7.2 0.9 bitcast_dynamic-update-slice_fusion.4
  8.1 0.9 bitcast_dynamic-update-slice_fusion.3
  9.0 0.9 bitcast_dynamic-update-slice_fusion.2
  10.0 0.9 bitcast_dynamic-update-slice_fusion.1
  10.9 0.9 bitcast_dynamic-update-slice_fusion
  11.8 0.7 broadcast_dynamic-update-slice_fusion
  12.5 0.0 copy-start.1
  12.5 0.9 copy-done.1
  13.4 0.0 all-gather.2.cloned.1.call-update
  13.4 0.0 copy-start.2
  13.4 0.0 copy-start.3
  13.5 0.0 copy-start.5
  13.5 0.0 copy-start.4
  13.5 5.3 %all-to-all-start = ((f32[8,32,2048]{2,1,0:T(8,128)}), f32[8,32,2048]{2,1,0:T(8,128)S(1)}, u32[]{:S(2)}, u32[]{:S(2)}) async-start(f32[8,32,2048]{2,1,0:T(8,128)} %bitcast.102), calls=%async_computation | async-start | bytes 4194304 | tf_op jit(solution)/shard_map/all_to_all | solution.py:40
  18.8 0.0 copy-done.2
  18.8 0.1 dynamic_slice.10
  18.9 0.0 copy-done.3
  18.9 0.0 copy-done.5
  18.9 0.1 select_reduce_fusion
  19.0 0.1 dynamic_slice.11
  19.1 0.1 compare_reduce_fusion.15
  19.2 34.6 %all-to-all-done = f32[8,32,2048]{2,1,0:T(8,128)S(1)} async-done(((f32[8,32,2048]{2,1,0:T(8,128)}), f32[8,32,2048]{2,1,0:T(8,128)S(1)}, u32[]{:S(2)}, u32[]{:S(2)}) %all-to-all-start) | async-done | bytes 2097184 | tf_op jit(solution)/shard_map/all_to_all | solution.py:40
  53.8 1.3 copy-done
  55.1 2.2 %copy.17 = f32[4,8,8,2048]{3,1,2,0:T(8,128)S(1)} copy(f32[4,8,8,2048]{3,1,0,2:T(8,128)} %bitcast.101) | data formatting | bytes 4194304
  57.3 19.5 %all-gather.2.cloned.1.call-done = f32[6,16,16384]{2,1,0:T(8,128)} async-done(((f32[6,16,2048]{2,1,0:T(8,128)}), f32[6,16,16384]{2,1,0:T(8,128)}) %all-gather.2.cloned.1.call-update) | async-done | bytes 6291472 | tf_op jit(solution)/shard_map/all_gather | solution.py:82
  76.8 5.8 %fusion.2 = (f32[1,1,16384]{2,1,0:T(1,128)S(1)}, f32[1,1,16384]{2,1,0:T(1,128)S(1)}, f32[1,1,16384]{2,1,0:T(1,128)S(1)}, f32[1,1,16384]{2,1,0:T(1,128)S(1)}, f32...) fusion(f32[6,16,16384]{2,1,0:T(8,128)} %all-gather.2.cloned.1.c, ...), kind=kLoop, calls=%fused_computation.62 | loop fusion | bytes 2490368 | tf_op jit(solution)/shard_map/slice | solution.py:54
  82.7 5.7 %fusion.3 = (f32[1,1,16384]{2,1,0:T(1,128)S(1)}, f32[1,1,16384]{2,1,0:T(1,128)S(1)}, f32[1,1,16384]{2,1,0:T(1,128)S(1)}, f32[1,1,16384]{2,1,0:T(1,128)S(1)}, f32...) fusion(f32[6,16,16384]{2,1,0:T(8,128)} %all-gather.2.cloned.1.c, ...), kind=kLoop, calls=%fused_computation.63 | loop fusion | bytes 2490368 | tf_op jit(solution)/shard_map/slice | solution.py:54
  88.4 5.5 %fusion.1 = (f32[1,1,16384]{2,1,0:T(1,128)S(1)}, f32[1,1,16384]{2,1,0:T(1,128)S(1)}, f32[1,1,16384]{2,1,0:T(1,128)S(1)}, f32[1,1,16384]{2,1,0:T(1,128)S(1)}, f32...) fusion(f32[6,16,16384]{2,1,0:T(8,128)} %all-gather.2.cloned.1.c, ...), kind=kLoop, calls=%fused_computation.61 | loop fusion | bytes 2490368 | tf_op jit(solution)/shard_map/slice | solution.py:54
  94.1 6.1 %fusion = (f32[1,1,16384]{2,1,0:T(1,128)S(1)}, f32[1,1,16384]{2,1,0:T(1,128)S(1)}, f32[1,1,16384]{2,1,0:T(1,128)S(1)}, f32[1,1,16384]{2,1,0:T(1,128)S(1)}, f32[1...) fusion(f32[6,16,16384]{2,1,0:T(8,128)} %all-gather.2.cloned.1.c, ...), kind=kLoop, calls=%fused_computation.60 | loop fusion | bytes 2490368 | tf_op jit(solution)/shard_map/slice | solution.py:54
  100.2 2.1 %fusion.4 = (f32[1,1,16384]{2,1,0:T(1,128)S(1)}, f32[1,1,16384]{2,1,0:T(1,128)S(1)}, f32[1,1,16384]{2,1,0:T(1,128)S(1)}, f32[1,1,16384]{2,1,0:T(1,128)S(1)}, f32[1,1,16384]{2,1,0:T(1,128)S(1)}) fusion(f32[6,16,16384]{2,1,0:T(8,128)} %all-gather.2.cloned.1.call-done), kind=kLoop, calls=%fused_computation.64 | loop fusion | bytes 655360 | tf_op jit(solution)/shard_map/slice | solution.py:54
  102.4 1.4 maximum_select_fusion.15
  103.8 1.4 maximum_select_fusion.14
  105.2 1.4 maximum_select_fusion.13
  106.6 1.4 maximum_select_fusion.12
  107.9 1.6 maximum_select_fusion.11
  109.5 1.4 maximum_select_fusion.10
  110.9 1.4 maximum_select_fusion.9
  112.3 1.4 maximum_select_fusion.8
  113.7 1.4 maximum_select_fusion.7
  115.1 1.4 maximum_select_fusion.6
  116.5 1.4 maximum_select_fusion.5
  117.9 1.4 maximum_select_fusion.4
  119.3 1.4 maximum_select_fusion.3
  120.6 1.6 maximum_select_fusion.2
  122.2 1.4 maximum_select_fusion.1
  123.6 3.4 %multiply_reduce_fusion = (f32[]{:T(128)}, f32[32]{0:T(128)}, f32[32,16384]{1,0:T(8,128)}) fusion(f32[16384]{0:T(1024)S(1)} %bitcast.169, f32[32]{0:T(128)S(1)} %dynamic_slice.11, f32[16384]{0:T(1024)S(1)} %bitcast.170, f32[16384]{0:T(1024)S(1)} %bitcast.171, f32[32]{0:T(128)S(1)} %dynamic_slice.10, f32[16384]{0:T(1024)S(1)} %bitcast.108, ...), kind=kLoop, calls=%fused_computation.16 | loop fusion | flops 7339999 | bytes 4653476 | tf_op jit(solution)/shard_map/reduce_sum | solution.py:84
  127.0 39.5 %psum.7 = f32[]{:T(128)} all-reduce(f32[]{:T(128)} %get-tuple-element.3), channel_id=1, replica_groups=mesh['trade'=4,'node'=8] {'trade','node'}, use_global_device_ids=true, to_apply=%region_19.20 | all-reduce | flops 1 | bytes 8 | tf_op jit(solution)/shard_map/psum | solution.py:84
  (19 shorter events, 0.2 us)
Async XLA Ops:
  7.2 69.7 %all-gather.2.cloned.1.call-start = ((), (), s32[]{:S(2)}) async-start(), calls=%async_computation.1 | async-start | bytes 7077888 | tf_op jit(solution)/shard_map/all_gather | solution.py:82
  12.5 0.9 copy-start.1
  13.4 5.4 %copy-start.2 = (s32[256]{0:T(256)S(1)}, s32[256]{0:T(256)}, u32[]{:S(2)}) copy-start(s32[256]{0:T(256)} %param.20) | copy-start | bytes 3076
  13.4 5.5 %copy-start.3 = (s32[256]{0:T(256)S(1)}, s32[256]{0:T(256)}, u32[]{:S(2)}) copy-start(s32[256]{0:T(256)} %param.19) | copy-start | bytes 3076
  13.5 5.5 %copy-start.5 = (f32[64]{0:T(128)S(1)}, f32[64]{0:T(128)}, u32[]{:S(2)}) copy-start(f32[64]{0:T(128)} %param.21) | copy-start | bytes 772
  13.5 5.6 %copy-start.4 = (s32[256,4]{0,1:T(4,128)S(1)}, s32[256,4]{0,1:T(4,128)}, u32[]{:S(2)}) copy-start(s32[256,4]{0,1:T(4,128)} %param.18) | copy-start | bytes 12292
  13.5 40.3 %all-to-all-start = ((f32[8,32,2048]{2,1,0:T(8,128)}), f32[8,32,2048]{2,1,0:T(8,128)S(1)}, u32[]{:S(2)}, u32[]{:S(2)}) async-start(f32[8,32,2048]{2,1,0:T(8,128)} %bitcast.102), calls=%async_computation | async-start | bytes 4194304 | tf_op jit(solution)/shard_map/all_to_all | solution.py:40
  53.8 1.3 copy-start
Sparse Core Ops, SparseCore 0:
  13.6 63.2 all-gather.1
where the time goes:
time: 176 us; the launch traced here: 175 us
  waiting for transfers between devices  54.1 us (31%)
  blocking collectives  39.5 us (22%)
  local copies, waits for them, and re-layouts  35.1 us (20%)
  other arithmetic  24.9 us (14%)
  between operations  16.2 us (9%)
  starting transfers between devices  5.38 us (3%)
    psum x1, blocking collectives, local(): lax.psum(jnp.sum(prices), ('trade', 'node')) / values_in.shape[0]  39.5 us
    all_to_all x1, waiting for transfers between devices, to_trade_rows(): lax.all_to_all(blocks, 'node', split_axis=0, concat_axis=2, tiled=True)  34.6 us
    select_n x15, other arithmetic, exercise(): return jnp.where(active[:, None], jnp.maximum(values, payoff), values)  21.1 us
    all_gather x1, waiting for transfers between devices, local(): lattice = lax.all_gather(local_lattice, 'node', axis=2, tiled=True)  19.5 us
    slice x3, local copies, waits for them, and re-layouts, roll_back(): lattice[2, local_step]  14 us
    slice x2, local copies, waits for them, and re-layouts, roll_back(): lattice[0, local_step]  11.2 us
    unnamed x18, local copies, waits for them, and re-layouts  9.01 us
    all_to_all x1, starting transfers between devices, to_trade_rows(): lax.all_to_all(blocks, 'node', split_axis=0, concat_axis=2, tiled=True)  5.34 us
  transfers between devices with their start and end apart: 2, of which 2 were waited for; matrix products, arithmetic and copies ran while one was open for 1% of the time, Pallas kernels for 0%

commit v1 on v0

v1 whole, which is shorter than its diff:
```python
import functools
import jax
import jax.numpy as jnp
from jax import lax
from jax.experimental import pallas as pl
from jax.experimental.pallas import tpu as pltpu
from jax.sharding import PartitionSpec as P

LANES = 128
HALF = 64
SUB = 8
MESH = pl.DeviceIdType.MESH
NEVER = 1e30


def strikes_of(bucket, strike_table):
    levels = lax.broadcasted_iota(jnp.int32, (1, strike_table.shape[0]), 1)
    return jnp.sum(
        jnp.where(
            bucket[:, None] == levels, strike_table[None, :], jnp.zeros((), strike_table.dtype)
        ),
        axis=1,
    )


def flip(me, d, n):
    out = 0
    bit = 1
    while bit < n:
        mine, other = (me // bit) % 2, (d // bit) % 2
        out = out + bit * (mine + other - 2 * mine * other)
        bit *= 2
    return out


def kernel(
    n, m, steps, rows, width,
    values_ref, up_ref, down_ref, disc_ref, swap_ref, ann_ref, price_ref, table_ref,
    out_ref, small_ref,
    vals, halo_v, raw, halo_c, coef, res, pacc, pmsg, precv, ztot, zrecv,
    in_sem, hs_sem, hr_sem, send_sem, recv_sem, self_sem, zs_sem, zr_sem, ps_sem, pr_sem,
):
    t = lax.axis_index("trade")
    me = lax.axis_index("node")
    block = rows if rows < 16 else 16
    parts = rows // block
    groups = block // SUB
    tiles = width // LANES
    lattice = (up_ref, down_ref, disc_ref, swap_ref, ann_ref)

    loads = [pltpu.make_async_copy(values_ref, vals, in_sem.at[0])]
    for k, ref in enumerate(lattice):
        loads.append(pltpu.make_async_copy(ref, raw.at[k], in_sem.at[1 + k]))
    for copy in loads:
        copy.start()

    barrier = pltpu.get_barrier_semaphore()
    for d in range(1, n):
        pl.semaphore_signal(barrier, inc=1, device_id=(t, (me + d) % n), device_id_type=MESH)
    for d in range(1, m):
        pl.semaphore_signal(barrier, inc=1, device_id=((t + d) % m, me), device_id_type=MESH)
    pl.semaphore_wait(barrier, n + m - 2)

    sides = ((0, (me + n - 1) % n, 0), (1, (me + 1) % n, width - LANES))
    halos = []
    for slot, target, first in sides:
        for k, ref in enumerate(lattice):
            halos.append(pltpu.make_async_remote_copy(
                src_ref=ref.at[:, pl.ds(first, LANES)], dst_ref=halo_c.at[slot, k],
                send_sem=hs_sem.at[slot, k], recv_sem=hr_sem.at[slot, k],
                device_id=(t, target), device_id_type=MESH))
    for slot, target, first in sides:
        halos.append(pltpu.make_async_remote_copy(
            src_ref=values_ref.at[:, pl.ds(first, LANES)], dst_ref=halo_v.at[slot],
            send_sem=hs_sem.at[slot, 5], recv_sem=hr_sem.at[slot, 5],
            device_id=(t, target), device_id_type=MESH))
    for copy in halos:
        copy.start()

    pmsg[...] = jnp.zeros_like(pmsg)

    def put_coefs(source, columns):
        up, down, disc, swap, ann = source
        rows_of = (disc * up, disc * (1.0 - up - down), disc * down, ann * swap, ann)
        for s in range(steps):
            for k in range(5):
                row = rows_of[k][s:s + 1, :]
                coef[s, k, :, columns] = jnp.broadcast_to(row, (SUB, row.shape[1]))

    for copy in loads[1:]:
        copy.wait()
    for i in range(tiles):
        cols = slice(i * LANES, (i + 1) * LANES)
        put_coefs([raw[k, :, cols] for k in range(5)], cols)
    loads[0].wait()

    lane = lax.broadcasted_iota(jnp.int32, (SUB, LANES), 1)
    has_right = jnp.where(me < n - 1, 1, 0)
    has_left = jnp.where(me > 0, 1, 0)

    def halo_mask(shape):
        at = lax.broadcasted_iota(jnp.int32, shape, 1)
        return jnp.where(at < HALF, has_right, has_left) > 0, at < HALF

    for copy in halos:
        copy.wait_recv()
    inside, right = halo_mask((steps, LANES))
    put_coefs(
        [jnp.where(inside, jnp.where(right, halo_c[0, k], halo_c[1, k]), 0.0) for k in range(5)],
        slice(width, width + LANES),
    )
    inside, right = halo_mask((SUB, LANES))
    first_lane = lane == 0
    last_lane = lane == LANES - 1

    def roll_block(row):
        start, tabs = [], []
        for g in range(groups):
            at = pl.ds(pl.multiple_of(row + g * SUB, SUB), SUB)
            line = [vals[at, i * LANES:(i + 1) * LANES] for i in range(tiles)]
            line.append(jnp.where(inside, jnp.where(right, halo_v[0, at, :], halo_v[1, at, :]), 0.0))
            start.append(line)
            tabs.append(table_ref[at, :])

        def step(s, carry):
            lines, tabs = carry
            new_lines, new_tabs = [], []
            for g in range(groups):
                sign = jnp.broadcast_to(tabs[g][:, 0:1], (SUB, LANES))
                level = jnp.broadcast_to(tabs[g][:, HALF:HALF + 1], (SUB, LANES))
                new_tabs.append(pltpu.roll(tabs[g], LANES - 1, 1))
                line = lines[g]
                ahead = [pltpu.roll(v, LANES - 1, 1) for v in line]
                behind = [pltpu.roll(v, 1, 1) for v in line]
                new = []
                for i in range(tiles + 1):
                    cols = slice(i * LANES, (i + 1) * LANES)
                    above = jnp.where(last_lane, ahead[(i + 1) % (tiles + 1)], ahead[i])
                    below = jnp.where(first_lane, behind[i - 1], behind[i])
                    rolled = (
                        coef[s, 0, :, cols] * above
                        + coef[s, 1, :, cols] * line[i]
                        + coef[s, 2, :, cols] * below
                    )
                    payoff = sign * coef[s, 3, :, cols] - level * coef[s, 4, :, cols]
                    new.append(jnp.maximum(rolled, payoff))
                new_lines.append(new)
            return new_lines, new_tabs

        lines, _ = lax.fori_loop(0, steps, step, (start, tabs))
        for g in range(groups):
            at = pl.ds(pl.multiple_of(row + g * SUB, SUB), SUB)
            total = jnp.zeros((SUB, LANES), jnp.float32)
            for i in range(tiles):
                cols = slice(i * LANES, (i + 1) * LANES)
                res[at, cols] = lines[g][i]
                total = total + lines[g][i] * price_ref[0:1, cols]
            pacc[at, :] = total

    def remote(d, h):
        dest = flip(me, d, n)
        return pltpu.make_async_remote_copy(
            src_ref=res.at[pl.ds(pl.multiple_of(dest * rows + h * block, SUB), block), :],
            dst_ref=out_ref.at[pl.ds(h * block, block), pl.ds(pl.multiple_of(me * width, LANES), width)],
            send_sem=send_sem.at[d, h], recv_sem=recv_sem.at[d, h],
            device_id=(t, dest), device_id_type=MESH)

    def at_home(h):
        return pltpu.make_async_copy(
            res.at[pl.ds(pl.multiple_of(me * rows + h * block, SUB), block), :],
            out_ref.at[pl.ds(h * block, block), pl.ds(pl.multiple_of(me * width, LANES), width)],
            self_sem.at[h])

    order = sum(d * 8 ** p for p, d in enumerate((2, 4, 3, 5, 6, 7, 1, 0)))

    def one_partner(p, code):
        d = code % 8 if n == 8 else (p + 2) % n
        dest = flip(me, d, n)
        for h in range(parts):
            roll_block(dest * rows + h * block)

            @pl.when(d > 0)
            def _():
                remote(d, h).start()

            @pl.when(d == 0)
            def _():
                at_home(h).start()
        return code // 8

    lax.fori_loop(0, n, one_partner, jnp.int32(order if n == 8 else 0))

    total = jnp.zeros((SUB, LANES), jnp.float32)
    for g in range(n * rows // SUB):
        total = total + pacc[g * SUB:(g + 1) * SUB, :]
    ztot[...] = total
    zcopies = []
    for d in range(1, m):
        zcopies.append(pltpu.make_async_remote_copy(
            src_ref=ztot, dst_ref=zrecv.at[d - 1],
            send_sem=zs_sem.at[d - 1], recv_sem=zr_sem.at[d - 1],
            device_id=((t + d) % m, me), device_id_type=MESH))
    for copy in zcopies:
        copy.start()
    ones = jnp.ones((SUB, LANES), jnp.float32)
    for d in range(n):
        dest = flip(me, d, n)
        mine = pacc[pl.ds(pl.multiple_of(dest * rows, SUB), rows), :]
        pmsg[d, 0:SUB, 0:rows] = lax.dot_general(
            ones, mine, (((1,), (1,)), ((), ())),
            precision=lax.Precision.HIGHEST, preferred_element_type=jnp.float32)
    for copy in zcopies:
        copy.wait_recv()
    for d in range(1, m):
        total = total + zrecv[d - 1]
    for d in range(n):
        pmsg[d, SUB:2 * SUB, :] = total
    pcopies = []
    for d in range(1, n):
        pcopies.append(pltpu.make_async_remote_copy(
            src_ref=pmsg.at[d], dst_ref=precv.at[d - 1],
            send_sem=ps_sem.at[d - 1], recv_sem=pr_sem.at[d - 1],
            device_id=(t, flip(me, d, n)), device_id_type=MESH))
    for copy in pcopies:
        copy.start()
    both = pmsg[0]
    for d, copy in enumerate(pcopies):
        copy.wait_recv()
        both = both + precv[d]
    small_ref[0:SUB, :] = both[0:SUB]
    small_ref[SUB:2 * SUB, :] = jnp.broadcast_to(
        jnp.sum(both[SUB:2 * SUB], keepdims=True) / (n * rows), (SUB, LANES))

    def drain(d, _):
        for h in range(parts):
            remote(d, h).wait()
        return 0

    lax.fori_loop(1, n, drain, 0)
    for h in range(parts):
        at_home(h).wait()
    for copy in halos + zcopies + pcopies:
        copy.wait_send()


def local(
    values_in, prob_up, prob_down, discount, swap_rate, annuity, state_price,
    exercise_step, strike_bucket, notional_sign, strike_table,
):
    n, m = lax.axis_size("node"), lax.axis_size("trade")
    steps = prob_up.shape[0]
    trades, width = values_in.shape
    rows = trades // n
    assert steps <= HALF and n & (n - 1) == 0
    block = min(rows, 16)

    strike = strikes_of(strike_bucket, strike_table)
    signs = (2 * notional_sign - 1).astype(jnp.float32)
    at = lax.broadcasted_iota(jnp.int32, (1, LANES), 1)
    active = jnp.any(exercise_step[:, :, None] == (at % HALF)[None], axis=1)
    table = jnp.where(
        at < HALF,
        jnp.where(active, signs[:, None], 0.0),
        jnp.where(active, (signs * strike)[:, None], NEVER),
    )

    hbm = pl.BlockSpec(memory_space=pl.ANY)
    vmem = pl.BlockSpec(memory_space=pltpu.VMEM)
    dma = pltpu.SemaphoreType.DMA
    f32 = jnp.float32
    out, small = pl.pallas_call(
        functools.partial(kernel, n, m, steps, rows, width),
        out_shape=(
            jax.ShapeDtypeStruct((rows, n * width), f32),
            jax.ShapeDtypeStruct((2 * SUB, LANES), f32),
        ),
        in_specs=[hbm] * 6 + [vmem] * 2,
        out_specs=(hbm, vmem),
        scratch_shapes=[
            pltpu.VMEM((trades, width), f32),
            pltpu.VMEM((2, trades, LANES), f32),
            pltpu.VMEM((5, steps, width), f32),
            pltpu.VMEM((2, 5, steps, LANES), f32),
            pltpu.VMEM((steps, 5, SUB, width + LANES), f32),
            pltpu.VMEM((trades, width), f32),
            pltpu.VMEM((trades, LANES), f32),
            pltpu.VMEM((n, 2 * SUB, LANES), f32),
            pltpu.VMEM((n - 1, 2 * SUB, LANES), f32),
            pltpu.VMEM((SUB, LANES), f32),
            pltpu.VMEM((m - 1, SUB, LANES), f32),
            dma((6,)), dma((2, 6)), dma((2, 6)),
            dma((n, rows // block)), dma((n, rows // block)), dma((rows // block,)),
            dma((m - 1,)), dma((m - 1,)), dma((n - 1,)), dma((n - 1,)),
        ],
        compiler_params=pltpu.CompilerParams(
            collective_id=0, has_side_effects=True, vmem_limit_bytes=40 * 1024 * 1024
        ),
        name="rollback",
    )(values_in, prob_up, prob_down, discount, swap_rate, annuity, state_price[None, :], table)
    return out, small[0, :rows], small[SUB, 0]


def solution(mesh):
    in_specs = (
        P("trade", "node"),
        P(None, "node"),
        P(None, "node"),
        P(None, "node"),
        P(None, "node"),
        P(None, "node"),
        P("node"),
        P("trade", None),
        P("trade"),
        P("trade"),
        P(),
    )
    out_specs = (P(("trade", "node"), None), P(("trade", "node")), P())
    return jax.shard_map(local, mesh=mesh, in_specs=in_specs, out_specs=out_specs, check_vma=False)
```

time: 176 us -> 73.6 us (0.42)
  Pallas kernels: 0 us -> 60.3 us
  waiting for transfers between devices: 54.1 us -> 0 us
  blocking collectives: 39.5 us -> 0 us
  local copies, waits for them, and re-layouts: 35.1 us -> 9.14 us
  other arithmetic: 24.9 us -> 3.2 us
  between operations: 16.2 us -> 0.68 us
  starting transfers between devices: 5.38 us -> 0 us
    pallas_call x0 -> x1, Pallas kernels: none -> 60.3 us  [local(): pl.pallas_call(functools.partial(kernel, n, m, steps, rows, width), out_s...]
    psum x1 -> x0, blocking collectives: 39.5 us -> none  [local(): lax.psum(jnp.sum(prices), ('trade', 'node')) / values_in.shape[0]]
    all_to_all x1 -> x0, waiting for transfers between devices: 34.6 us -> none  [to_trade_rows(): lax.all_to_all(blocks, 'node', split_axis=0, concat_axis=2, tiled=True)]
    slice x5 -> x1, local copies, waits for them, and re-layouts: 25.2 us -> 0.51 us  [local(): return (out, small[0, :rows], small[SUB, 0])]
    select_n x15 -> x2, other arithmetic: 21.1 us -> 0.14 us  [the longest x1 0.13 us: local(): jnp.where(at < HALF, jnp.where(active, signs[:, None], 0.0), jnp.where(ac...]
    all_gather x1 -> x0, waiting for transfers between devices: 19.5 us -> none  [local(): lattice = lax.all_gather(local_lattice, 'node', axis=2, tiled=True)]
    all_to_all x1 -> x0, starting transfers between devices: 5.34 us -> none  [to_trade_rows(): lax.all_to_all(blocks, 'node', split_axis=0, concat_axis=2, tiled=True)]
    reduce_sum x1 -> x0, other arithmetic: 3.38 us -> none  [local(): jnp.sum(prices)]
  transfers between devices with their start and end apart: 2 -> 0, of which waited for: 2 -> 0; matrix products, arithmetic and copies ran while one was open for 1% -> 0% of each run, Pallas kernels for 0% -> 0%
where the time goes in v1:
time: 73.6 us; the launch traced here: 73.3 us
  Pallas kernels  60.3 us (82%)
  local copies, waits for them, and re-layouts  9.14 us (12%)
  other arithmetic  3.2 us (4%)
    pallas_call x1, Pallas kernels, local(): pl.pallas_call(functools.partial(kernel, n, m, steps, rows, width), out_s...  60.3 us
    unnamed x15, local copies, waits for them, and re-layouts  8.12 us

profile of v1, /device:TPU:0, one launch (start us, length us, event | category | flops | bytes accessed | tf_op | source)
XLA Modules:
  0.0 73.3 jit_solution(5468046424703382501)
XLA Ops:
  0.6 0.9 %compare_reduce_fusion = pred[256,128]{1,0:T(8,128)(4,1)S(1)} fusion(s32[128]{0:T(128)S(1)} %and_select_fusion, s32[256,4]{0,1:T(4,128)} %param.18), kind=kLoop, calls=%fused_computation | loop fusion | flops 229376 | bytes 37376 | tf_op jit(solution)/shard_map/reduce_or | solution.py:260
  1.5 0.8 %select_reduce_fusion = f32[256]{0:T(256)S(1)} fusion(f32[64]{0:T(128)} %param.21, s32[256]{0:T(256)} %param.19), kind=kLoop, calls=%fused_computation.2 | loop fusion | flops 48896 | bytes 2304 | tf_op jit(solution)/shard_map/reduce_sum | solution.py:18
  2.3 0.7 fusion
  3.0 0.7 add_convert_fusion
  3.7 0.1 select_select_fusion.table_ref
  3.9 0.0 copy-start
  3.9 1.6 %copy-done = f32[256,2048]{1,0:T(8,128)S(1)} copy-done((f32[256,2048]{1,0:T(8,128)S(1)}, f32[256,2048]{1,0:T(8,128)}, u32[]{:S(2)}) %copy-start) | copy-done | bytes 2097176
  5.4 0.0 copy-start.1
  5.4 0.9 %copy-done.1 = f32[16,2048]{1,0:T(8,128)S(1)} copy-done((f32[16,2048]{1,0:T(8,128)S(1)}, f32[16,2048]{1,0:T(8,128)}, u32[]{:S(2)}) %copy-start.1) | copy-done | bytes 131096
  6.3 0.0 copy-start.2
  6.4 0.9 %copy-done.2 = f32[16,2048]{1,0:T(8,128)S(1)} copy-done((f32[16,2048]{1,0:T(8,128)S(1)}, f32[16,2048]{1,0:T(8,128)}, u32[]{:S(2)}) %copy-start.2) | copy-done | bytes 131096
  7.3 0.0 copy-start.3
  7.3 0.9 %copy-done.3 = f32[16,2048]{1,0:T(8,128)S(1)} copy-done((f32[16,2048]{1,0:T(8,128)S(1)}, f32[16,2048]{1,0:T(8,128)}, u32[]{:S(2)}) %copy-start.3) | copy-done | bytes 131096
  8.2 0.0 copy-start.4
  8.2 0.9 %copy-done.4 = f32[16,2048]{1,0:T(8,128)S(1)} copy-done((f32[16,2048]{1,0:T(8,128)S(1)}, f32[16,2048]{1,0:T(8,128)}, u32[]{:S(2)}) %copy-start.4) | copy-done | bytes 131096
  9.1 0.0 copy-start.5
  9.1 0.9 %copy-done.5 = f32[16,2048]{1,0:T(8,128)S(1)} copy-done((f32[16,2048]{1,0:T(8,128)S(1)}, f32[16,2048]{1,0:T(8,128)}, u32[]{:S(2)}) %copy-start.5) | copy-done | bytes 131096
  10.0 0.0 copy-start.6
  10.0 0.7 copy-done.6
  10.7 60.3 %rollback.1 = (f32[32,16384]{1,0:T(8,128)S(1)}, f32[16,128]{1,0:T(8,128)S(1)}) custom-call(f32[256,2048]{1,0:T(8,128)S(1)} %copy-done, f32[16,2048]{1,0:T(8,128)S(1)} %copy-done.1, f32[16,2048]{1,0:T(8,128)S(1)} %copy-done.2, f32[16,2048]{1,0:T(8,128)S(1)} %copy-done.3, f32[16,2048]{1,0:T(8,128)S(1)} %copy-done.4, f32[16,2048]{1,0:T(8,128)S(1)} %copy-done.5, ...), custom_call_target="tpu_custom_call" | custom-call | tf_op jit(solution)/shard_map/rollback/pallas_call | solution.py:271
  70.9 0.5 slice.7
  71.4 0.5 slice_bitcast_fusion
  72.0 1.3 %copy.16 = f32[32,16384]{1,0:T(8,128)} copy(f32[32,16384]{1,0:T(8,128)S(1)} %get-tuple-element.10) | data formatting | bytes 4194304
  (2 shorter events, 0.0 us)
Async XLA Ops:
  3.9 1.6 %copy-start = (f32[256,2048]{1,0:T(8,128)S(1)}, f32[256,2048]{1,0:T(8,128)}, u32[]{:S(2)}) copy-start(f32[256,2048]{1,0:T(8,128)} %values_ref.1) | copy-start | bytes 6291460
  5.4 0.9 %copy-start.1 = (f32[16,2048]{1,0:T(8,128)S(1)}, f32[16,2048]{1,0:T(8,128)}, u32[]{:S(2)}) copy-start(f32[16,2048]{1,0:T(8,128)} %up_ref.1) | copy-start | bytes 393220
  6.3 0.9 %copy-start.2 = (f32[16,2048]{1,0:T(8,128)S(1)}, f32[16,2048]{1,0:T(8,128)}, u32[]{:S(2)}) copy-start(f32[16,2048]{1,0:T(8,128)} %down_ref.1) | copy-start | bytes 393220
  7.3 0.9 %copy-start.3 = (f32[16,2048]{1,0:T(8,128)S(1)}, f32[16,2048]{1,0:T(8,128)}, u32[]{:S(2)}) copy-start(f32[16,2048]{1,0:T(8,128)} %disc_ref.1) | copy-start | bytes 393220
  8.2 0.9 %copy-start.4 = (f32[16,2048]{1,0:T(8,128)S(1)}, f32[16,2048]{1,0:T(8,128)}, u32[]{:S(2)}) copy-start(f32[16,2048]{1,0:T(8,128)} %swap_ref.1) | copy-start | bytes 393220
  9.1 0.9 %copy-start.5 = (f32[16,2048]{1,0:T(8,128)S(1)}, f32[16,2048]{1,0:T(8,128)}, u32[]{:S(2)}) copy-start(f32[16,2048]{1,0:T(8,128)} %ann_ref.1) | copy-start | bytes 393220
  10.0 0.7 copy-start.6

commit v2 on v1

--- a/solution.py
+++ b/solution.py
@@ -147,7 +147,7 @@
                 new_lines.append(new)
             return new_lines, new_tabs
 
-        lines, _ = lax.fori_loop(0, steps, step, (start, tabs))
+        lines, _ = lax.fori_loop(0, steps, step, (start, tabs), unroll=4)
         for g in range(groups):
             at = pl.ds(pl.multiple_of(row + g * SUB, SUB), SUB)
             total = jnp.zeros((SUB, LANES), jnp.float32)
@@ -264,7 +264,8 @@
         jnp.where(active, (signs * strike)[:, None], NEVER),
     )
 
-    hbm = pl.BlockSpec(memory_space=pl.ANY)
+    hbm = pl.BlockSpec(memory_space=pltpu.HBM)
+    either = pl.BlockSpec(memory_space=pl.ANY)
     vmem = pl.BlockSpec(memory_space=pltpu.VMEM)
     dma = pltpu.SemaphoreType.DMA
     f32 = jnp.float32
@@ -275,7 +276,7 @@
             jax.ShapeDtypeStruct((2 * SUB, LANES), f32),
         ),
         in_specs=[hbm] * 6 + [vmem] * 2,
-        out_specs=(hbm, vmem),
+        out_specs=(either, vmem),
         scratch_shapes=[
             pltpu.VMEM((trades, width), f32),
             pltpu.VMEM((2, trades, LANES), f32),

time: 73.6 us -> 69.7 us (0.947)
  Pallas kernels: 60.3 us -> 56.3 us
    pallas_call x1, Pallas kernels: 60.3 us -> 56.3 us  [local(): pl.pallas_call(functools.partial(kernel, n, m, steps, rows, width), out_s...]
where the time goes in v2:
time: 69.7 us; the launch traced here: 69.3 us
  Pallas kernels  56.3 us (81%)
  local copies, waits for them, and re-layouts  9.14 us (13%)
  other arithmetic  3.2 us (5%)
    pallas_call x1, Pallas kernels, local(): pl.pallas_call(functools.partial(kernel, n, m, steps, rows, width), out_s...  56.3 us
    unnamed x15, local copies, waits for them, and re-layouts  8.12 us

profile of v2, /device:TPU:0, one launch (start us, length us, event | category | flops | bytes accessed | tf_op | source)
XLA Modules:
  0.0 69.3 jit_solution(14076777921397091418)
XLA Ops:
  0.6 0.9 %compare_reduce_fusion = pred[256,128]{1,0:T(8,128)(4,1)S(1)} fusion(s32[128]{0:T(128)S(1)} %and_select_fusion, s32[256,4]{0,1:T(4,128)} %param.18), kind=kLoop, calls=%fused_computation | loop fusion | flops 229376 | bytes 37376 | tf_op jit(solution)/shard_map/reduce_or | solution.py:260
  1.5 0.8 %select_reduce_fusion = f32[256]{0:T(256)S(1)} fusion(f32[64]{0:T(128)} %param.21, s32[256]{0:T(256)} %param.19), kind=kLoop, calls=%fused_computation.2 | loop fusion | flops 48896 | bytes 2304 | tf_op jit(solution)/shard_map/reduce_sum | solution.py:18
  2.3 0.7 fusion
  3.0 0.7 add_convert_fusion
  3.7 0.1 select_select_fusion.table_ref
  3.9 0.0 copy-start
  3.9 1.6 %copy-done = f32[256,2048]{1,0:T(8,128)S(1)} copy-done((f32[256,2048]{1,0:T(8,128)S(1)}, f32[256,2048]{1,0:T(8,128)}, u32[]{:S(2)}) %copy-start) | copy-done | bytes 2097176
  5.4 0.0 copy-start.1
  5.4 0.9 %copy-done.1 = f32[16,2048]{1,0:T(8,128)S(1)} copy-done((f32[16,2048]{1,0:T(8,128)S(1)}, f32[16,2048]{1,0:T(8,128)}, u32[]{:S(2)}) %copy-start.1) | copy-done | bytes 131096
  6.3 0.0 copy-start.2
  6.4 0.9 %copy-done.2 = f32[16,2048]{1,0:T(8,128)S(1)} copy-done((f32[16,2048]{1,0:T(8,128)S(1)}, f32[16,2048]{1,0:T(8,128)}, u32[]{:S(2)}) %copy-start.2) | copy-done | bytes 131096
  7.3 0.0 copy-start.3
  7.3 0.9 %copy-done.3 = f32[16,2048]{1,0:T(8,128)S(1)} copy-done((f32[16,2048]{1,0:T(8,128)S(1)}, f32[16,2048]{1,0:T(8,128)}, u32[]{:S(2)}) %copy-start.3) | copy-done | bytes 131096
  8.2 0.0 copy-start.4
  8.2 0.9 %copy-done.4 = f32[16,2048]{1,0:T(8,128)S(1)} copy-done((f32[16,2048]{1,0:T(8,128)S(1)}, f32[16,2048]{1,0:T(8,128)}, u32[]{:S(2)}) %copy-start.4) | copy-done | bytes 131096
  9.1 0.0 copy-start.5
  9.1 0.9 %copy-done.5 = f32[16,2048]{1,0:T(8,128)S(1)} copy-done((f32[16,2048]{1,0:T(8,128)S(1)}, f32[16,2048]{1,0:T(8,128)}, u32[]{:S(2)}) %copy-start.5) | copy-done | bytes 131096
  10.0 0.0 copy-start.6
  10.0 0.7 %copy-done.6 = f32[2048]{0:T(1024)S(1)} copy-done((f32[2048]{0:T(1024)S(1)}, f32[2048]{0:T(1024)}, u32[]{:S(2)}) %copy-start.6) | copy-done | bytes 8216
  10.7 56.3 %rollback.1 = (f32[32,16384]{1,0:T(8,128)S(1)}, f32[16,128]{1,0:T(8,128)S(1)}) custom-call(f32[256,2048]{1,0:T(8,128)S(1)} %copy-done, f32[16,2048]{1,0:T(8,128)S(1)} %copy-done.1, f32[16,2048]{1,0:T(8,128)S(1)} %copy-done.2, f32[16,2048]{1,0:T(8,128)S(1)} %copy-done.3, f32[16,2048]{1,0:T(8,128)S(1)} %copy-done.4, f32[16,2048]{1,0:T(8,128)S(1)} %copy-done.5, ...), custom_call_target="tpu_custom_call" | custom-call | tf_op jit(solution)/shard_map/rollback/pallas_call | solution.py:272
  67.0 0.5 slice.7
  67.5 0.5 slice_bitcast_fusion
  68.0 1.3 %copy.16 = f32[32,16384]{1,0:T(8,128)} copy(f32[32,16384]{1,0:T(8,128)S(1)} %get-tuple-element.10) | data formatting | bytes 4194304
  (2 shorter events, 0.0 us)
Async XLA Ops:
  3.9 1.6 %copy-start = (f32[256,2048]{1,0:T(8,128)S(1)}, f32[256,2048]{1,0:T(8,128)}, u32[]{:S(2)}) copy-start(f32[256,2048]{1,0:T(8,128)} %values_ref.1) | copy-start | bytes 6291460
  5.4 0.9 %copy-start.1 = (f32[16,2048]{1,0:T(8,128)S(1)}, f32[16,2048]{1,0:T(8,128)}, u32[]{:S(2)}) copy-start(f32[16,2048]{1,0:T(8,128)} %up_ref.1) | copy-start | bytes 393220
  6.3 0.9 %copy-start.2 = (f32[16,2048]{1,0:T(8,128)S(1)}, f32[16,2048]{1,0:T(8,128)}, u32[]{:S(2)}) copy-start(f32[16,2048]{1,0:T(8,128)} %down_ref.1) | copy-start | bytes 393220
  7.3 0.9 %copy-start.3 = (f32[16,2048]{1,0:T(8,128)S(1)}, f32[16,2048]{1,0:T(8,128)}, u32[]{:S(2)}) copy-start(f32[16,2048]{1,0:T(8,128)} %disc_ref.1) | copy-start | bytes 393220
  8.2 0.9 %copy-start.4 = (f32[16,2048]{1,0:T(8,128)S(1)}, f32[16,2048]{1,0:T(8,128)}, u32[]{:S(2)}) copy-start(f32[16,2048]{1,0:T(8,128)} %swap_ref.1) | copy-start | bytes 393220
  9.1 0.9 %copy-start.5 = (f32[16,2048]{1,0:T(8,128)S(1)}, f32[16,2048]{1,0:T(8,128)}, u32[]{:S(2)}) copy-start(f32[16,2048]{1,0:T(8,128)} %ann_ref.1) | copy-start | bytes 393220
  10.0 0.7 %copy-start.6 = (f32[2048]{0:T(1024)S(1)}, f32[2048]{0:T(1024)}, u32[]{:S(2)}) copy-start(f32[2048]{0:T(1024)} %param.17) | copy-start | bytes 24580
